TPU v7x, 32 devices: a whole 2x2x4 slice. The times are simulated.
32 devices in a mesh: node: 8 (over z, x), freq: 4 (over y, core).
Axes of the slice: x: 2, y: 2, z: 4, core: 2. Of those that a mesh axis runs over, the one named last changes fastest.
Arguments:
- action_old: float32 [36, 36, 4096], P('freq', None, 'node'), may hold values from 0.05 to 2
- source: float32 [36, 36, 4096], P('freq', None, 'node'), may hold values from -4 to 4
- time_weight: float32 [4096], P('node'), may hold values from 0.5 to 4
- group_speed: float32 [36], P('freq'), may hold values from 0.3 to 3
- normals: float32 [2, 8, 4096], P(None, None, 'node'), may hold values from -3 to 3
- refract: float32 [4096], P('node'), may hold values from -4 to 4
- freq_shift: float32 [4096], P('node'), may hold values from -4 to 4
- nbr_list: int32 [8, 6], P('node'), may hold values from -1 to 7, as said below
- send_nodes: int32 [8, 6, 32], P('node'), may hold values from 0 to 511, as said below
- adjacency: int32 [8, 4096], P(None, 'node'), may hold values from 0 to 703, as said below
Outputs:
- action_new: float32 [36, 36, 4096], P('freq', None, 'node')
Inputs may be any that keep to these rules, and one draw needn't show every extreme that they name: `nbr_list`: slot entries of subdomain p are distinct subdomains (p + o) or (p - o) modulo the number of subdomains, 1 <= o <= 3, or -1 for an empty slot; p + 1 and p - 1 are always listed; if p lists q then q lists p. `send_nodes`: local node indices of the sending subdomain. `adjacency`: entries as in the first step; an entry at or above 512 never names an empty slot.
All inputs are finite; a program needn't handle non-finite values.
Results may differ from a plain program's by a relative error of at most 0.000088.
Values sent between devices are 32-bit elements; how exact they have to be, the bound alone decides.
No kernel may reach another device: no remote copies, remote signals or barrier semaphores. Data moves between devices by JAX's collectives and lax.ppermute only.
A program may use at most 128 MiB of HBM per device.

v0:
```python
import functools
import math

import jax
import jax.numpy as jnp
import numpy as np
from jax import lax
from jax.experimental import pallas as pl
from jax.experimental.pallas import tpu as pltpu
from jax.sharding import PartitionSpec as P


REACH = 3
ITERS = 3
TILE = 256


def up_to(value, multiple):
    return -(-value // multiple) * multiple


def node_routes(count):
    masks = {p ^ ((p + d) % count) for p in range(count) for d in range(1, REACH + 1)}
    if count & (count - 1) == 0 and len(masks) <= 2 * REACH:
        order = [m for m in (6, 7, 2, 3, 5, 1) if m in masks]
        return [("xor", m) for m in order + sorted(masks - set(order))]
    routes = []
    for d in range(REACH, 0, -1):
        step = d & -d
        if count % (2 * step) == 0 and count > 2 * d:
            routes += [("swap", d, step, 0), ("swap", d, step, 1)]
        else:
            routes += [("shift", d), ("shift", -d)]
    return routes


def target_of(route, place, count):
    if route[0] == "xor":
        return place ^ route[1]
    if route[0] == "shift":
        return (place + route[1] + count) % count
    _, d, step, side = route
    turn = 1 - 2 * (((place // step) % 2) ^ side)
    return (place + turn * d + count) % count


def source_of(route, place, count):
    if route[0] == "shift":
        return target_of(("shift", -route[1]), place, count)
    return target_of(route, place, count)


def plan_of(routes):
    if routes[:2] == [("xor", 6), ("xor", 7)] and routes[-1] == ("xor", 1):
        groups = [[0, 1]] + [[j] for j in range(2, len(routes))]
        return groups, (0, len(groups) - 1)
    return [[j] for j in range(len(routes))], None


def band_routes(count):
    first = [(p ^ 1) if (p ^ 1) < count else p for p in range(count)]
    second = [p if p == 0 else p + (1 if p % 2 else -1) for p in range(count)]
    second = [q if q < count else p for p, q in enumerate(second)]
    if count % 2 == 0:
        second[0], second[-1] = count - 1, 0
    return [first, second]


def split(values):
    high = values.astype(jnp.bfloat16)
    low = (values - high.astype(jnp.float32)).astype(jnp.bfloat16)
    return high, low


def hot(index, first, rows):
    step = min(rows, 256)
    shape = (step, index.shape[1])
    ids = lax.broadcasted_iota(jnp.int32, shape, 0).astype(jnp.float32).astype(jnp.bfloat16)
    blocks = []
    for start in range(0, rows, step):
        offset = (index - (first + start)).astype(jnp.float32).astype(jnp.bfloat16)
        hits = ids == jnp.broadcast_to(offset, shape)
        blocks.append(jnp.where(hits, jnp.bfloat16(1), jnp.bfloat16(0)))
    return blocks[0] if len(blocks) == 1 else jnp.concatenate(blocks, axis=0)


def dot(left, right, contract=((1,), (0,))):
    return lax.dot_general(left, right, (contract, ((), ())), preferred_element_type=jnp.float32)


def store_groups(rows, get, bands, angles, unit):
    for g in range(0, bands, unit):
        values = [get(f) for f in range(g, min(g + unit, bands))]
        block = values[0] if len(values) == 1 else jnp.concatenate(values, axis=0)
        tail = up_to(block.shape[0], 8) - block.shape[0]
        if tail:
            block = jnp.concatenate([block, jnp.zeros((tail, block.shape[1]), jnp.float32)], axis=0)
        high, low = split(block)
        window = slice(g * angles, g * angles + block.shape[0])
        rows[0, window, : block.shape[1]] = high
        rows[1, window, : block.shape[1]] = low


def emit(rows, picks, even, fields, parcels, edges):
    local = fields.shape[2]
    nt = ((1,), (1,))
    chosen = picks[...]
    out = dot(chosen, rows[0, :, :local], nt) + dot(chosen, rows[1, :, :local], nt)
    start = 0
    for parcel in parcels:
        parcel[...] = out[start : start + parcel.shape[0], :]
        start += parcel.shape[0]
    last, first = fields[fields.shape[0] - 1], fields[0]
    edges[0][...] = jnp.where(even, last, first)
    edges[1][...] = jnp.where(even, first, last)


def clear_tail(rows, used):
    start = used // 16 * 16
    rows[:, start:, :] = jnp.zeros((2, rows.shape[1] - start, rows.shape[2]), rows.dtype)


def slopes(normals, trig, k, lo, hi):
    x = normals[0, k : k + 1, lo:hi]
    y = normals[1, k : k + 1, lo:hi]
    return trig[0] * x + trig[1] * y


WEIGHT, REFRACT, SHIFT, EVEN, RISE, FALL, TABLE = 0, 1, 2, 3, 4, 5, 8


def prep_kernel(
    action,
    near,
    sends_in,
    adjacency_in,
    normals_in,
    weight,
    refract,
    shift,
    trig_in,
    *refs,
    routes,
    columns_of,
    groups_out,
    axes,
    unit,
):
    node, freq, count, groups = axes
    total = len(routes)
    parcels, refs = refs[:groups_out], refs[groups_out:]
    edges, refs = refs[:2], refs[2:]
    picks, fields, index_out, normals, nodal, trig = refs[:6]
    rows, neighbours, sends, adjacency, raw, line, arrived, small = refs[6:]
    bands, angles, local = fields.shape
    slots, width = sends.shape[0], sends.shape[2]
    pairs = [
        (near, neighbours),
        (sends_in, sends),
        (adjacency_in, adjacency),
        (normals_in, raw),
        (weight, nodal.at[pl.ds(WEIGHT, 1)]),
        (refract, nodal.at[pl.ds(REFRACT, 1)]),
        (shift, nodal.at[pl.ds(SHIFT, 1)]),
        (trig_in, line),
    ]
    little = [pltpu.make_async_copy(x, y, small.at[i]) for i, (x, y) in enumerate(pairs)]
    copies = [
        pltpu.make_async_copy(action.at[f], fields.at[f], arrived.at[f]) for f in range(bands)
    ]
    for copy in little[:2] + copies + little[2:]:
        copy.start()
    place, band = lax.axis_index(node), lax.axis_index(freq)
    clear_tail(rows, bands * angles)
    for copy in little[:2]:
        copy.wait()
    near_of = [neighbours[0, s] for s in range(slots)]
    table = []
    for route in routes:
        target = target_of(route, place, count)
        slot = jnp.int32(0)
        for s in range(slots):
            slot = jnp.where(near_of[s] == target, s, slot)
        table.append(sends[slot].astype(jnp.float32))
    height = up_to(total, 8)
    if height > total:
        table.append(jnp.zeros((height - total, width), jnp.float32))
    table = jnp.concatenate(table, axis=0)
    if width % 128:
        spare = jnp.zeros((height, up_to(width, 128) - width), jnp.float32)
        table = jnp.concatenate([table, spare], axis=1)
    columns = table.T.astype(jnp.int32)
    lanes = lax.broadcasted_iota(jnp.int32, (width, local), 1)
    for j in range(total):
        hits = lanes == columns[:width, j : j + 1]
        picks[j * width : (j + 1) * width, :] = jnp.where(hits, 1.0, 0.0).astype(jnp.bfloat16)

    def get(f):
        copies[f].wait()
        return fields[f]

    store_groups(rows, get, bands, angles, unit)
    is_even = jnp.full((1, local), band % 2, jnp.int32) == 0
    emit(rows, picks, is_even, fields, parcels, edges)
    for copy in little[2:]:
        copy.wait()
    entry = adjacency[...]
    index = entry
    for s in range(slots):
        column = jnp.int32(0)
        for r, c in zip(routes, columns_of):
            column = jnp.where(near_of[s] == source_of(r, place, count), c, column)
        inside = (entry >= local + s * width) & (entry < local + (s + 1) * width)
        index = jnp.where(inside, entry + column - s * width, index)
    index_out[...] = index
    used = entry != lax.broadcasted_iota(jnp.int32, entry.shape, 1)
    for i in range(2):
        normals[i] = jnp.where(used, raw[i], 0.0)
        trig[i] = jnp.broadcast_to(line[i], trig.shape[1:])
    moved = nodal[SHIFT : SHIFT + 1]
    has_below = jnp.where(band > 0, 1.0, 0.0)
    has_above = jnp.where(band < groups - 1, 1.0, 0.0)
    nodal[EVEN : EVEN + 1] = jnp.where(is_even, 1.0, 0.0)
    nodal[RISE : RISE + 1] = jnp.maximum(moved, 0.0) * has_below
    nodal[FALL : FALL + 1] = jnp.maximum(-moved, 0.0) * has_above
    nodal[FALL + 1 :] = jnp.zeros((TABLE - FALL - 1, local), jnp.float32)


def stack_parcels(stack, halos, arrivals, width):
    depth = stack.shape[1] // 2
    blocks = [halos[g][row : row + width, :] for g, row in arrivals]
    if depth > len(blocks) * width:
        spare = depth - len(blocks) * width
        blocks.append(jnp.zeros((spare, blocks[0].shape[1]), jnp.float32))
    high, low = split(jnp.concatenate(blocks, axis=0).T)
    stack[:, :depth] = high
    stack[:, depth:] = low


def gathered(acc, rows, stack, index, normals, trig, first, bands, angles, unit, finish):
    local = index.shape[1]
    total = up_to(bands * angles, 8)
    waiting = []
    for lo in range(0, local, TILE):
        hi = min(lo + TILE, local)
        for k in range(index.shape[0]):
            entry = index[k : k + 1, lo:hi]
            terms = []
            if rows is not None:
                onehot = hot(entry, 0, local)
                terms += [dot(rows[i, :total, :local], onehot) for i in range(2)]
            if stack is not None:
                onehot = hot(entry, first, stack.shape[1] // 2)
                terms.append(dot(stack[:total], jnp.concatenate([onehot, onehot], axis=0)))
            values = functools.reduce(jnp.add, terms)
            weight = jnp.maximum(-slopes(normals, trig, k, lo, hi), 0.0)
            for g in range(0, bands, unit):
                height = up_to(min(unit, bands - g) * angles, 8)
                window = slice(g * angles, g * angles + height)
                piece = weight[:height] * values[window]
                if k:
                    piece = piece + acc[window, lo:hi]
                acc[window, lo:hi] = piece
            for _ in range(-(-bands // index.shape[0])):
                if waiting:
                    finish(*waiting.pop(0))
        for item in waiting:
            finish(*item)
        waiting = [(f, lo, hi) for f in range(bands)]
    for item in waiting:
        finish(*item)


def local_kernel(*refs, first, arrivals, groups, width, unit):
    halos, refs = refs[:groups], refs[groups:]
    stack = None
    if arrivals:
        stack, refs = refs[-1], refs[:-1]
    if first:
        (action, source_hbm, speeds_hbm, index, normals, nodal, trig) = refs[:7]
        part, invd, invs, base, rows, acc, source, speeds, arrived, came = refs[7:]
        copy = pltpu.make_async_copy(source_hbm, source, arrived)
        copy.start()
        fetch = pltpu.make_async_copy(speeds_hbm, speeds, came)
        fetch.start()
    else:
        (action, invd, invs, base, index, normals, nodal, trig) = refs[:8]
        part, rows, acc = refs[8:]
    bands, angles, local = action.shape
    store_groups(rows, lambda f: action[f], bands, angles, unit)
    if arrivals:
        stack_parcels(stack, halos, arrivals, width)

    def finish(f, lo, hi):
        if first and (f, lo) == (0, 0):
            copy.wait()
            fetch.wait()
        here = action[f, :, lo:hi]
        shift = nodal[SHIFT : SHIFT + 1, lo:hi]
        turning = nodal[REFRACT : REFRACT + 1, lo:hi] * trig[0, :angles, : hi - lo]
        if first:
            outflow = jnp.zeros((angles, hi - lo), jnp.float32)
            wave = [trig[i, :angles, : hi - lo] for i in range(2)]
            weight = nodal[WEIGHT : WEIGHT + 1, lo:hi]
            if f == 0:
                for k in range(index.shape[0]):
                    outflow = outflow + jnp.maximum(slopes(normals, wave, k, lo, hi), 0.0)
                kept[lo] = (outflow, weight + jnp.abs(turning) + jnp.abs(shift))
            outflow, fixed = kept[lo]
            inv = 1.0 / (fixed + speeds[0, f] * outflow)
            start = (weight * here + source[f, :, lo:hi]) * inv
            scaled = speeds[0, f] * inv
            invd[f, :, lo:hi] = inv
            invs[f, :, lo:hi] = scaled
            base[f, :, lo:hi] = start
        else:
            inv, scaled, start = invd[f, :, lo:hi], invs[f, :, lo:hi], base[f, :, lo:hi]
        before = jnp.concatenate([here[angles - 1 :], here[: angles - 1]], axis=0)
        after = jnp.concatenate([here[1:], here[:1]], axis=0)
        inflow = jnp.maximum(turning, 0.0) * before + jnp.maximum(-turning, 0.0) * after
        if f > 0:
            inflow = inflow + jnp.maximum(shift, 0.0) * action[f - 1, :, lo:hi]
        if f < bands - 1:
            inflow = inflow + jnp.maximum(-shift, 0.0) * action[f + 1, :, lo:hi]
        edges = acc[f * angles : (f + 1) * angles, lo:hi]
        part[f, :, lo:hi] = start + inflow * inv + edges * scaled

    kept = {}
    gathered(acc, rows, stack, index, normals, trig, local, bands, angles, unit, finish)


def halo_kernel(*refs, groups, arrivals, first, width, last, unit):
    halos, refs = refs[:groups], refs[groups:]
    (edge_a, edge_b, part, invd, invs, index, normals, nodal, trig), refs = refs[:9], refs[9:]
    if last:
        out, acc, stack = refs
    else:
        picks, out = refs[:2]
        parcels, edges, (acc, stack, rows) = refs[2:-5], refs[-5:-3], refs[-3:]
    bands, angles, _ = part.shape
    stack_parcels(stack, halos, arrivals, width)
    is_even = nodal[EVEN : EVEN + 1, :] > 0.5

    def finish(f, lo, hi):
        value = part[f, :, lo:hi] + acc[f * angles : (f + 1) * angles, lo:hi] * invs[f, :, lo:hi]
        even = is_even[:, lo:hi]
        if f == 0:
            below = jnp.where(even, edge_b[:, lo:hi], edge_a[:, lo:hi])
            value = value + nodal[RISE : RISE + 1, lo:hi] * below * invd[f, :, lo:hi]
        if f == bands - 1:
            above = jnp.where(even, edge_a[:, lo:hi], edge_b[:, lo:hi])
            value = value + nodal[FALL : FALL + 1, lo:hi] * above * invd[f, :, lo:hi]
        out[f, :, lo:hi] = value

    gathered(acc, None, stack, index, normals, trig, first, bands, angles, unit, finish)
    if not last:
        clear_tail(rows, bands * angles)
        store_groups(rows, lambda f: out[f], bands, angles, unit)
        emit(rows, picks, is_even, out, parcels, edges)


def body(
    action_old,
    source,
    time_weight,
    group_speed,
    normals,
    refract,
    freq_shift,
    nbr_list,
    send_nodes,
    adjacency,
):
    bands, angles, local = action_old.shape
    slots, width = send_nodes.shape[1:]
    degree = adjacency.shape[0]
    count = lax.axis_size("node")
    groups = lax.axis_size("freq")
    routes = node_routes(count)
    edge_routes = band_routes(groups)
    plan, relay = plan_of(routes)
    total = len(routes)
    arrivals = [(g, place * width) for g, group in enumerate(plan) for place in range(len(group))]
    if relay:
        arrivals[1] = (relay[1], width)
    early = [
        j
        for j in range(total)
        if relay and routes[j] in (("xor", 6), ("xor", 2))
    ]
    late = [j for j in range(total) if j not in early]
    margin = up_to(len(early) * width, 128)
    columns_of = [
        early.index(j) * width if j in early else margin + late.index(j) * width
        for j in range(total)
    ]
    unit = 8 // math.gcd(angles, 8)
    lanes = up_to(bands * angles, 128)

    theta = 2.0 * math.pi * np.arange(angles).astype(np.float32) / angles
    trig = np.stack([np.cos(theta), np.sin(theta)]).astype(np.float32)[:, :, None]
    trig = jnp.asarray(np.concatenate([trig] * unit, axis=1))

    f32, i32, bf16 = jnp.float32, jnp.int32, jnp.bfloat16
    shape = jax.ShapeDtypeStruct
    cube = shape((bands, angles, local), f32)
    outgoing = [shape((width * len(group), lanes), f32) for group in plan]
    outgoing += [shape((angles, local), f32)] * 2
    tables = [
        shape((total * width, local), bf16),
        cube,
        shape((degree, local), i32),
        shape((2, degree, local), f32),
        shape((TABLE, local), f32),
        shape((2, unit * angles, TILE), f32),
    ]
    rows = pltpu.VMEM((2, lanes, local), bf16)

    def stack(members):
        return pltpu.VMEM((lanes, 2 * up_to(len(members) * width, 128)), bf16)

    def places(members):
        used = sorted({arrivals[j][0] for j in members})
        return used, [(used.index(arrivals[j][0]), arrivals[j][1]) for j in members]

    early_groups, early_arrivals = places(early)
    late_groups, late_arrivals = places(late)
    acc = pltpu.VMEM((up_to(bands * angles, 8), local), f32)
    dma = pltpu.SemaphoreType.DMA
    vmem = pl.BlockSpec(memory_space=pltpu.VMEM)
    far = pl.BlockSpec(memory_space=pltpu.HBM)
    params = pltpu.CompilerParams(vmem_limit_bytes=24 * 2**20)

    def call(kernel, arrays, outs, scratch, depth_rows, distant=(), **options):
        flops = 4 * bands * angles * depth_rows * degree * local
        arrays = [
            pltpu.with_memory_space_constraint(x, pltpu.HBM) if i in distant else x
            for i, x in enumerate(arrays)
        ]
        return pl.pallas_call(
            functools.partial(kernel, unit=unit, **options),
            in_specs=[far if i in distant else vmem for i in range(len(arrays))],
            out_specs=[vmem] * len(outs),
            out_shape=outs,
            scratch_shapes=scratch,
            compiler_params=params,
            cost_estimate=pl.CostEstimate(
                flops=flops, transcendentals=0, bytes_accessed=4 * bands * angles * local
            ),
        )(*arrays)

    nodal = [x.reshape(1, local) for x in (time_weight, refract, freq_shift)]
    prepared = call(
        prep_kernel,
        [action_old, nbr_list, send_nodes.reshape(slots, 1, width), adjacency, normals, *nodal, trig],
        outgoing + tables,
        [
            rows,
            pltpu.SMEM((1, slots), i32),
            pltpu.VMEM((slots, 1, width), i32),
            pltpu.VMEM((degree, local), i32),
            pltpu.VMEM((2, degree, local), f32),
            pltpu.VMEM(trig.shape, f32),
            dma((bands,)),
            dma((8,)),
        ],
        0,
        distant=range(9),
        routes=routes,
        columns_of=columns_of,
        groups_out=len(plan),
        axes=("node", "freq", count, groups),
    )
    sends = prepared[: len(outgoing)]
    picks, spectra, *shared = prepared[len(outgoing) :]

    def along(block, group):
        route = routes[plan[group][0]]
        return lax.ppermute(block, "node", [(p, target_of(route, p, count)) for p in range(count)])

    for step in range(ITERS):
        direct = [g for g in range(len(plan)) if not relay or g != relay[1]]
        arrived = {}
        for g in direct:
            arrived[g] = along(sends[g], g)
        across = [
            lax.ppermute(x, "freq", list(enumerate(r)))
            for x, r in zip(sends[len(plan) :], edge_routes)
        ]
        if relay:
            passed = jnp.concatenate([sends[relay[1]], arrived[relay[0]][width:]], axis=0)
            passed, spectra = lax.optimization_barrier((passed, spectra))
            arrived[relay[1]] = along(passed, relay[1])
        ahead = [arrived[g] for g in early_groups]
        after = [arrived[g] for g in late_groups] + across
        window = dict(arrivals=early_arrivals, groups=len(early_groups), width=width)
        stacks = [stack(early)] if early else []
        depth = local + margin // 2
        if step == 0:
            part, invd, invs, base = call(
                local_kernel,
                [*ahead, spectra, source, group_speed.reshape(1, bands), *shared],
                [cube] * 4,
                [
                    rows,
                    acc,
                    pltpu.VMEM((bands, angles, local), f32),
                    pltpu.SMEM((1, bands), f32),
                    dma,
                    dma,
                    *stacks,
                ],
                depth,
                distant=(len(ahead) + 1, len(ahead) + 2),
                first=True,
                **window,
            )
        else:
            (part,) = call(
                local_kernel,
                [*ahead, spectra, invd, invs, base, *shared],
                [cube],
                [rows, acc, *stacks],
                depth,
                first=False,
                **window,
            )
        last = step == ITERS - 1
        spectra, *sends = call(
            halo_kernel,
            [*after, part, invd, invs, *shared] + ([] if last else [picks]),
            [cube] + ([] if last else outgoing),
            [acc, stack(late)] + ([] if last else [rows]),
            up_to(len(late) * width, 128),
            groups=len(late_groups),
            arrivals=late_arrivals,
            first=local + margin,
            width=width,
            last=last,
        )
    return spectra


def solution(mesh):
    in_specs = (
        P("freq", None, "node"),
        P("freq", None, "node"),
        P("node"),
        P("freq"),
        P(None, None, "node"),
        P("node"),
        P("node"),
        P("node", None),
        P("node", None, None),
        P(None, "node"),
    )
    out_specs = P("freq", None, "node")
    return jax.shard_map(body, mesh=mesh, in_specs=in_specs, out_specs=out_specs, check_vma=False)
```

profile of v0, /device:TPU:0, one launch (start us, length us, event | category | flops | bytes accessed | tf_op | source)
XLA Modules:
  0.0 54.2 jit_solution(12721872382990583912)
XLA Ops:
  0.0 1.9 %shard_map.109 = (f32[64,384]{1,0:T(8,128)S(1)}, f32[32,384]{1,0:T(8,128)S(1)}, f32[32,384]{1,0:T(8,128)S(1)}, f32[32,384]{1,0:T(8,128)S(1)}, f32[32,384]{1,0:T(...) custom-call(f32[9,36,512]{2,1,0:T(8,128)} %action.1, ...), custom_call_target="tpu_custom_call" | custom-call | bytes 663552 | tf_op jit(solution)/shard_map/pallas_call | solution.py:440
  1.9 5.1 %collective-permute-start.2 = (f32[64,384]{1,0:T(8,128)S(1)}, f32[64,384]{1,0:T(8,128)S(1)}, u32[]{:S(2)}, u32[]{:S(2)}) collective-permute-start(f32[64,384]{1,0:T(8,128)S(1)} %get-tuple-element.47), channel_id=1, source_target_pairs={{0,24},{4,28},{8,16},{12,20},{16,8},{20,12},{24,0},{28,4},{1,25},{... | collective-permute-start | bytes 294920 | tf_op jit(solution)/shard_map/ppermute | solution.py:479
  7.1 0.5 collective-permute-start
  7.5 1.1 %collective-permute-start.1 = (f32[32,384]{1,0:T(8,128)S(1)}, f32[32,384]{1,0:T(8,128)S(1)}, u32[]{:S(2)}, u32[]{:S(2)}) collective-permute-start(f32[32,384]{1,0:T(8,128)S(1)} %get-tuple-element.45), channel_id=1, source_target_pairs={{0,20},{4,16},{8,28},{12,24},{16,4},{20,0},{24,12},{28,8},{1,21},{... | collective-permute-start | bytes 147464 | tf_op jit(solution)/shard_map/ppermute | solution.py:479
  8.6 1.4 %collective-permute-start.6 = (f32[32,384]{1,0:T(8,128)S(1)}, f32[32,384]{1,0:T(8,128)S(1)}, u32[]{:S(2)}, u32[]{:S(2)}) collective-permute-start(f32[32,384]{1,0:T(8,128)S(1)} %get-tuple-element.52), channel_id=1, source_target_pairs={{0,8},{4,12},{8,0},{12,4},{16,24},{20,28},{24,16},{28,20},{1,9},{5... | collective-permute-start | bytes 147464 | tf_op jit(solution)/shard_map/ppermute | solution.py:479
  10.0 0.0 collective-permute-start.4
  10.0 0.4 collective-permute-done.2.refs_0_
  10.4 1.2 %collective-permute-start.5 = (f32[36,512]{1,0:T(8,128)S(1)}, f32[36,512]{1,0:T(8,128)S(1)}, u32[]{:S(2)}, u32[]{:S(2)}) collective-permute-start(f32[36,512]{1,0:T(8,128)S(1)} %get-tuple-element.51), channel_id=1, source_target_pairs={{0,3},{1,2},{2,1},{3,0},{4,7},{5,6},{6,5},{7,4},{8,11},{9,10},{10,... | collective-permute-start | bytes 221192 | tf_op jit(solution)/shard_map/ppermute | solution.py:487
  11.7 1.9 %collective-permute-done.6.refs_1_ = f32[32,384]{1,0:T(8,128)S(1)} collective-permute-done((f32[32,384]{1,0:T(8,128)S(1)}, f32[32,384]{1,0:T(8,128)S(1)}, u32[]{:S(2)}, u32[]{:S(2)}) %collective-permute-start.6) | collective-permute-done | bytes 49184 | tf_op jit(solution)/shard_map/ppermute | solution.py:479
  13.6 1.1 %collective-permute-start.3 = (f32[64,384]{1,0:T(8,128)S(1)}, f32[64,384]{1,0:T(8,128)S(1)}, u32[]{:S(2)}, u32[]{:S(2)}) collective-permute-start(f32[64,384]{1,0:T(8,128)S(1)} %pad_maximum_fusion), channel_id=1, source_target_pairs={{0,4},{4,0},{8,12},{12,8},{16,20},{20,16},{24,28},{28,24},{1,5},{5... | collective-permute-start | bytes 294920 | tf_op jit(solution)/shard_map/ppermute | solution.py:479
  14.7 5.1 %shard_map.110 = (f32[9,36,512]{2,1,0:T(8,128)S(1)}, f32[9,36,512]{2,1,0:T(8,128)S(1)}, f32[9,36,512]{2,1,0:T(8,128)S(1)}, f32[9,36,512]{2,1,0:T(8,128)S(1)}) custom-call(f32[64,384]{1,0:T(8,128)S(1)} %collective-permute-done.2.refs_0_, f32[32,384]{1,0:T(8,128)S(1)} %collective-permute-done.6.refs_1_, f32[9,36,512]{2,1,0:T(8,128)S(1)} %get-tuple-element.53.refs_2_, ...), custom_call_target="tpu_custom_call" | custom-call | flops 3057647616 | bytes 663552 | tf_op jit(solution)/shard_map/pallas_call | solution.py:440
  19.8 0.0 collective-permute-done.refs_0_
  19.8 0.0 collective-permute-done.1.refs_1_
  19.8 0.0 collective-permute-done.4.refs_3_
  19.8 0.0 collective-permute-done.5.refs_4_
  19.8 0.0 collective-permute-done.3.refs_2_
  19.8 1.5 %shard_map.111 = (f32[9,36,512]{2,1,0:T(8,128)S(1)}, f32[64,384]{1,0:T(8,128)S(1)}, f32[32,384]{1,0:T(8,128)S(1)}, f32[32,384]{1,0:T(8,128)S(1)}, f32[32,384]{1,...) custom-call(f32[32,384]{1,0:T(8,128)S(1)} %collective-permute-done.refs_0_, ...), custom_call_target="tpu_custom_call" | custom-call | flops 679477248 | bytes 663552 | tf_op jit(solution)/shard_map/pallas_call | solution.py:440
  21.3 3.3 %collective-permute-start.9 = (f32[64,384]{1,0:T(8,128)S(1)}, f32[64,384]{1,0:T(8,128)S(1)}, u32[]{:S(2)}, u32[]{:S(2)}) collective-permute-start(f32[64,384]{1,0:T(8,128)S(1)} %get-tuple-element.65), channel_id=1, source_target_pairs={{0,24},{4,28},{8,16},{12,20},{16,8},{20,12},{24,0},{28,4},{1,25},{... | collective-permute-start | bytes 294920 | tf_op jit(solution)/shard_map/ppermute | solution.py:479
  24.6 0.0 collective-permute-start.7
  24.6 2.1 %collective-permute-start.8 = (f32[32,384]{1,0:T(8,128)S(1)}, f32[32,384]{1,0:T(8,128)S(1)}, u32[]{:S(2)}, u32[]{:S(2)}) collective-permute-start(f32[32,384]{1,0:T(8,128)S(1)} %get-tuple-element.63), channel_id=1, source_target_pairs={{0,20},{4,16},{8,28},{12,24},{16,4},{20,0},{24,12},{28,8},{1,21},{... | collective-permute-start | bytes 147464 | tf_op jit(solution)/shard_map/ppermute | solution.py:479
  26.6 0.7 %collective-permute-start.13 = (f32[32,384]{1,0:T(8,128)S(1)}, f32[32,384]{1,0:T(8,128)S(1)}, u32[]{:S(2)}, u32[]{:S(2)}) collective-permute-start(f32[32,384]{1,0:T(8,128)S(1)} %get-tuple-element.70), channel_id=1, source_target_pairs={{0,8},{4,12},{8,0},{12,4},{16,24},{20,28},{24,16},{28,20},{1,9},{5... | collective-permute-start | bytes 147464 | tf_op jit(solution)/shard_map/ppermute | solution.py:479
  27.3 0.0 collective-permute-start.11
  27.3 0.5 collective-permute-done.9.refs_0_
  27.9 1.1 %collective-permute-start.12 = (f32[36,512]{1,0:T(8,128)S(1)}, f32[36,512]{1,0:T(8,128)S(1)}, u32[]{:S(2)}, u32[]{:S(2)}) collective-permute-start(f32[36,512]{1,0:T(8,128)S(1)} %get-tuple-element.69), channel_id=1, source_target_pairs={{0,3},{1,2},{2,1},{3,0},{4,7},{5,6},{6,5},{7,4},{8,11},{9,10},{10,... | collective-permute-start | bytes 221192 | tf_op jit(solution)/shard_map/ppermute | solution.py:487
  29.0 2.0 %collective-permute-done.13.refs_1_ = f32[32,384]{1,0:T(8,128)S(1)} collective-permute-done((f32[32,384]{1,0:T(8,128)S(1)}, f32[32,384]{1,0:T(8,128)S(1)}, u32[]{:S(2)}, u32[]{:S(2)}) %collective-permute-start.13) | collective-permute-done | bytes 49184 | tf_op jit(solution)/shard_map/ppermute | solution.py:479
  31.0 0.8 %collective-permute-start.10 = (f32[64,384]{1,0:T(8,128)S(1)}, f32[64,384]{1,0:T(8,128)S(1)}, u32[]{:S(2)}, u32[]{:S(2)}) collective-permute-start(f32[64,384]{1,0:T(8,128)S(1)} %pad_maximum_fusion.1), channel_id=1, source_target_pairs={{0,4},{4,0},{8,12},{12,8},{16,20},{20,16},{24,28},{28,24},{1,5},{5... | collective-permute-start | bytes 294920 | tf_op jit(solution)/shard_map/ppermute | solution.py:479
  31.8 4.1 %shard_map.112.refs_5_ = f32[9,36,512]{2,1,0:T(8,128)S(1)} custom-call(f32[64,384]{1,0:T(8,128)S(1)} %collective-permute-done.9.refs_0_, f32[32,384]{1,0:T(8,128)S(1)} %collective-permute-done.13.refs_1_, f32[9,36,512]{2,1,0:T(8,128)S(1)} %get-tuple-element.71.refs_2_, f32[9,36,512]{2,1,0:T(8,128)S(1)} %get-tuple-element.59.refs_6_.refs_3_, ...), custom_call_target="tpu_custom_call" | custom-call | flops 3057647616 | bytes 663552 | tf_op jit(solution)/shard_map/pallas_call | solution.py:440
  36.0 0.0 collective-permute-done.7.refs_0_
  36.0 0.0 collective-permute-done.8.refs_1_
  36.0 0.0 collective-permute-done.11.refs_3_
  36.0 0.0 collective-permute-done.12.refs_4_
  36.0 0.0 collective-permute-done.10.refs_2_
  36.0 1.5 %shard_map.113 = (f32[9,36,512]{2,1,0:T(8,128)S(1)}, f32[64,384]{1,0:T(8,128)S(1)}, f32[32,384]{1,0:T(8,128)S(1)}, f32[32,384]{1,0:T(8,128)S(1)}, f32[32,384]{1,...) custom-call(f32[32,384]{1,0:T(8,128)S(1)} %collective-permute-done.7.refs_0_, ...), custom_call_target="tpu_custom_call" | custom-call | flops 679477248 | bytes 663552 | tf_op jit(solution)/shard_map/pallas_call | solution.py:440
  37.5 2.7 %collective-permute-start.16 = (f32[64,384]{1,0:T(8,128)S(1)}, f32[64,384]{1,0:T(8,128)S(1)}, u32[]{:S(2)}, u32[]{:S(2)}) collective-permute-start(f32[64,384]{1,0:T(8,128)S(1)} %get-tuple-element.76), channel_id=1, source_target_pairs={{0,24},{4,28},{8,16},{12,20},{16,8},{20,12},{24,0},{28,4},{1,25},{... | collective-permute-start | bytes 294920 | tf_op jit(solution)/shard_map/ppermute | solution.py:479
  40.2 0.6 %collective-permute-start.14 = (f32[32,384]{1,0:T(8,128)S(1)}, f32[32,384]{1,0:T(8,128)S(1)}, u32[]{:S(2)}, u32[]{:S(2)}) collective-permute-start(f32[32,384]{1,0:T(8,128)S(1)} %get-tuple-element.73), channel_id=1, source_target_pairs={{0,12},{4,8},{8,4},{12,0},{16,28},{20,24},{24,20},{28,16},{1,13},{... | collective-permute-start | bytes 147464 | tf_op jit(solution)/shard_map/ppermute | solution.py:479
  40.8 2.1 %collective-permute-start.15 = (f32[32,384]{1,0:T(8,128)S(1)}, f32[32,384]{1,0:T(8,128)S(1)}, u32[]{:S(2)}, u32[]{:S(2)}) collective-permute-start(f32[32,384]{1,0:T(8,128)S(1)} %get-tuple-element.74), channel_id=1, source_target_pairs={{0,20},{4,16},{8,28},{12,24},{16,4},{20,0},{24,12},{28,8},{1,21},{... | collective-permute-start | bytes 147464 | tf_op jit(solution)/shard_map/ppermute | solution.py:479
  42.8 0.3 collective-permute-start.20
  43.2 0.0 collective-permute-start.18
  43.2 1.0 %collective-permute-done.16.refs_0_ = f32[64,384]{1,0:T(8,128)S(1)} collective-permute-done((f32[64,384]{1,0:T(8,128)S(1)}, f32[64,384]{1,0:T(8,128)S(1)}, u32[]{:S(2)}, u32[]{:S(2)}) %collective-permute-start.16) | collective-permute-done | bytes 98336 | tf_op jit(solution)/shard_map/ppermute | solution.py:479
  44.2 0.6 %collective-permute-start.19 = (f32[36,512]{1,0:T(8,128)S(1)}, f32[36,512]{1,0:T(8,128)S(1)}, u32[]{:S(2)}, u32[]{:S(2)}) collective-permute-start(f32[36,512]{1,0:T(8,128)S(1)} %get-tuple-element.80), channel_id=1, source_target_pairs={{0,3},{1,2},{2,1},{3,0},{4,7},{5,6},{6,5},{7,4},{8,11},{9,10},{10,... | collective-permute-start | bytes 221192 | tf_op jit(solution)/shard_map/ppermute | solution.py:487
  44.8 2.1 %collective-permute-done.20.refs_1_ = f32[32,384]{1,0:T(8,128)S(1)} collective-permute-done((f32[32,384]{1,0:T(8,128)S(1)}, f32[32,384]{1,0:T(8,128)S(1)}, u32[]{:S(2)}, u32[]{:S(2)}) %collective-permute-start.20) | collective-permute-done | bytes 49184 | tf_op jit(solution)/shard_map/ppermute | solution.py:479
  46.9 1.2 %collective-permute-start.17 = (f32[64,384]{1,0:T(8,128)S(1)}, f32[64,384]{1,0:T(8,128)S(1)}, u32[]{:S(2)}, u32[]{:S(2)}) collective-permute-start(f32[64,384]{1,0:T(8,128)S(1)} %pad_maximum_fusion.2), channel_id=1, source_target_pairs={{0,4},{4,0},{8,12},{12,8},{16,20},{20,16},{24,28},{28,24},{1,5},{5... | collective-permute-start | bytes 294920 | tf_op jit(solution)/shard_map/ppermute | solution.py:479
  48.1 4.1 %shard_map.114.refs_5_ = f32[9,36,512]{2,1,0:T(8,128)S(1)} custom-call(f32[64,384]{1,0:T(8,128)S(1)} %collective-permute-done.16.refs_0_, f32[32,384]{1,0:T(8,128)S(1)} %collective-permute-done.20.refs_1_, f32[9,36,512]{2,1,0:T(8,128)S(1)} %get-tuple-element.82.refs_2_, f32[9,36,512]{2,1,0:T(8,128)S(1)} %get-tuple-element.59.refs_6_.refs_3_, ...), custom_call_target="tpu_custom_call" | custom-call | flops 3057647616 | bytes 663552 | tf_op jit(solution)/shard_map/pallas_call | solution.py:440
  52.3 0.0 collective-permute-done.14.refs_0_
  52.3 0.0 collective-permute-done.15.refs_1_
  52.3 0.0 collective-permute-done.18.refs_3_
  52.3 0.0 collective-permute-done.19.refs_4_
  52.3 0.0 collective-permute-done.17.refs_2_
  52.3 1.9 %shard_map.115 = f32[9,36,512]{2,1,0:T(8,128)} custom-call(f32[32,384]{1,0:T(8,128)S(1)} %collective-permute-done.14.refs_0_, f32[32,384]{1,0:T(8,128)S(1)} %collective-permute-done.15.refs_1_, f32[64,384]{1,0:T(8,128)S(1)} %collective-permute-done.17.refs_2_, f32[36,512]{1,0:T(8,128)S(1)} %collective-permute-done.18.refs_3_, ...), custom_call_target="tpu_custom_call" | custom-call | flops 679477248 | bytes 663552 | tf_op jit(solution)/shard_map/pallas_call | solution.py:440
  (6 shorter events, 0.0 us)
Async XLA Ops:
  1.9 8.5 %collective-permute-start.2 = (f32[64,384]{1,0:T(8,128)S(1)}, f32[64,384]{1,0:T(8,128)S(1)}, u32[]{:S(2)}, u32[]{:S(2)}) collective-permute-start(f32[64,384]{1,0:T(8,128)S(1)} %get-tuple-element.47), channel_id=1, source_target_pairs={{0,24},{4,28},{8,16},{12,20},{16,8},{20,12},{24,0},{28,4},{1,25},{... | collective-permute-start | bytes 294920 | tf_op jit(solution)/shard_map/ppermute | solution.py:479
  7.1 12.7 %collective-permute-start = (f32[32,384]{1,0:T(8,128)S(1)}, f32[32,384]{1,0:T(8,128)S(1)}, u32[]{:S(2)}, u32[]{:S(2)}) collective-permute-start(f32[32,384]{1,0:T(8,128)S(1)} %get-tuple-element.44), channel_id=1, source_target_pairs={{0,12},{4,8},{8,4},{12,0},{16,28},{20,24},{24,20},{28,16},{1,13},{... | collective-permute-start | bytes 147464 | tf_op jit(solution)/shard_map/ppermute | solution.py:479
  7.5 12.3 %collective-permute-start.1 = (f32[32,384]{1,0:T(8,128)S(1)}, f32[32,384]{1,0:T(8,128)S(1)}, u32[]{:S(2)}, u32[]{:S(2)}) collective-permute-start(f32[32,384]{1,0:T(8,128)S(1)} %get-tuple-element.45), channel_id=1, source_target_pairs={{0,20},{4,16},{8,28},{12,24},{16,4},{20,0},{24,12},{28,8},{1,21},{... | collective-permute-start | bytes 147464 | tf_op jit(solution)/shard_map/ppermute | solution.py:479
  8.6 5.0 %collective-permute-start.6 = (f32[32,384]{1,0:T(8,128)S(1)}, f32[32,384]{1,0:T(8,128)S(1)}, u32[]{:S(2)}, u32[]{:S(2)}) collective-permute-start(f32[32,384]{1,0:T(8,128)S(1)} %get-tuple-element.52), channel_id=1, source_target_pairs={{0,8},{4,12},{8,0},{12,4},{16,24},{20,28},{24,16},{28,20},{1,9},{5... | collective-permute-start | bytes 147464 | tf_op jit(solution)/shard_map/ppermute | solution.py:479
  10.0 9.8 %collective-permute-start.4 = (f32[36,512]{1,0:T(8,128)S(1)}, f32[36,512]{1,0:T(8,128)S(1)}, u32[]{:S(2)}, u32[]{:S(2)}) collective-permute-start(f32[36,512]{1,0:T(8,128)S(1)} %get-tuple-element.50), channel_id=1, source_target_pairs={{0,1},{1,0},{2,3},{3,2},{4,5},{5,4},{6,7},{7,6},{8,9},{9,8},{10,11... | collective-permute-start | bytes 221192 | tf_op jit(solution)/shard_map/ppermute | solution.py:487
  10.4 9.4 %collective-permute-start.5 = (f32[36,512]{1,0:T(8,128)S(1)}, f32[36,512]{1,0:T(8,128)S(1)}, u32[]{:S(2)}, u32[]{:S(2)}) collective-permute-start(f32[36,512]{1,0:T(8,128)S(1)} %get-tuple-element.51), channel_id=1, source_target_pairs={{0,3},{1,2},{2,1},{3,0},{4,7},{5,6},{6,5},{7,4},{8,11},{9,10},{10,... | collective-permute-start | bytes 221192 | tf_op jit(solution)/shard_map/ppermute | solution.py:487
  13.6 6.2 %collective-permute-start.3 = (f32[64,384]{1,0:T(8,128)S(1)}, f32[64,384]{1,0:T(8,128)S(1)}, u32[]{:S(2)}, u32[]{:S(2)}) collective-permute-start(f32[64,384]{1,0:T(8,128)S(1)} %pad_maximum_fusion), channel_id=1, source_target_pairs={{0,4},{4,0},{8,12},{12,8},{16,20},{20,16},{24,28},{28,24},{1,5},{5... | collective-permute-start | bytes 294920 | tf_op jit(solution)/shard_map/ppermute | solution.py:479
  21.3 6.6 %collective-permute-start.9 = (f32[64,384]{1,0:T(8,128)S(1)}, f32[64,384]{1,0:T(8,128)S(1)}, u32[]{:S(2)}, u32[]{:S(2)}) collective-permute-start(f32[64,384]{1,0:T(8,128)S(1)} %get-tuple-element.65), channel_id=1, source_target_pairs={{0,24},{4,28},{8,16},{12,20},{16,8},{20,12},{24,0},{28,4},{1,25},{... | collective-permute-start | bytes 294920 | tf_op jit(solution)/shard_map/ppermute | solution.py:479
  24.6 11.4 %collective-permute-start.7 = (f32[32,384]{1,0:T(8,128)S(1)}, f32[32,384]{1,0:T(8,128)S(1)}, u32[]{:S(2)}, u32[]{:S(2)}) collective-permute-start(f32[32,384]{1,0:T(8,128)S(1)} %get-tuple-element.62), channel_id=1, source_target_pairs={{0,12},{4,8},{8,4},{12,0},{16,28},{20,24},{24,20},{28,16},{1,13},{... | collective-permute-start | bytes 147464 | tf_op jit(solution)/shard_map/ppermute | solution.py:479
  24.6 11.4 %collective-permute-start.8 = (f32[32,384]{1,0:T(8,128)S(1)}, f32[32,384]{1,0:T(8,128)S(1)}, u32[]{:S(2)}, u32[]{:S(2)}) collective-permute-start(f32[32,384]{1,0:T(8,128)S(1)} %get-tuple-element.63), channel_id=1, source_target_pairs={{0,20},{4,16},{8,28},{12,24},{16,4},{20,0},{24,12},{28,8},{1,21},{... | collective-permute-start | bytes 147464 | tf_op jit(solution)/shard_map/ppermute | solution.py:479
  26.6 4.3 %collective-permute-start.13 = (f32[32,384]{1,0:T(8,128)S(1)}, f32[32,384]{1,0:T(8,128)S(1)}, u32[]{:S(2)}, u32[]{:S(2)}) collective-permute-start(f32[32,384]{1,0:T(8,128)S(1)} %get-tuple-element.70), channel_id=1, source_target_pairs={{0,8},{4,12},{8,0},{12,4},{16,24},{20,28},{24,16},{28,20},{1,9},{5... | collective-permute-start | bytes 147464 | tf_op jit(solution)/shard_map/ppermute | solution.py:479
  27.3 8.7 %collective-permute-start.11 = (f32[36,512]{1,0:T(8,128)S(1)}, f32[36,512]{1,0:T(8,128)S(1)}, u32[]{:S(2)}, u32[]{:S(2)}) collective-permute-start(f32[36,512]{1,0:T(8,128)S(1)} %get-tuple-element.68), channel_id=1, source_target_pairs={{0,1},{1,0},{2,3},{3,2},{4,5},{5,4},{6,7},{7,6},{8,9},{9,8},{10,11... | collective-permute-start | bytes 221192 | tf_op jit(solution)/shard_map/ppermute | solution.py:487
  27.9 8.1 %collective-permute-start.12 = (f32[36,512]{1,0:T(8,128)S(1)}, f32[36,512]{1,0:T(8,128)S(1)}, u32[]{:S(2)}, u32[]{:S(2)}) collective-permute-start(f32[36,512]{1,0:T(8,128)S(1)} %get-tuple-element.69), channel_id=1, source_target_pairs={{0,3},{1,2},{2,1},{3,0},{4,7},{5,6},{6,5},{7,4},{8,11},{9,10},{10,... | collective-permute-start | bytes 221192 | tf_op jit(solution)/shard_map/ppermute | solution.py:487
  31.0 5.0 %collective-permute-start.10 = (f32[64,384]{1,0:T(8,128)S(1)}, f32[64,384]{1,0:T(8,128)S(1)}, u32[]{:S(2)}, u32[]{:S(2)}) collective-permute-start(f32[64,384]{1,0:T(8,128)S(1)} %pad_maximum_fusion.1), channel_id=1, source_target_pairs={{0,4},{4,0},{8,12},{12,8},{16,20},{20,16},{24,28},{28,24},{1,5},{5... | collective-permute-start | bytes 294920 | tf_op jit(solution)/shard_map/ppermute | solution.py:479
  37.5 6.7 %collective-permute-start.16 = (f32[64,384]{1,0:T(8,128)S(1)}, f32[64,384]{1,0:T(8,128)S(1)}, u32[]{:S(2)}, u32[]{:S(2)}) collective-permute-start(f32[64,384]{1,0:T(8,128)S(1)} %get-tuple-element.76), channel_id=1, source_target_pairs={{0,24},{4,28},{8,16},{12,20},{16,8},{20,12},{24,0},{28,4},{1,25},{... | collective-permute-start | bytes 294920 | tf_op jit(solution)/shard_map/ppermute | solution.py:479
  40.2 12.1 %collective-permute-start.14 = (f32[32,384]{1,0:T(8,128)S(1)}, f32[32,384]{1,0:T(8,128)S(1)}, u32[]{:S(2)}, u32[]{:S(2)}) collective-permute-start(f32[32,384]{1,0:T(8,128)S(1)} %get-tuple-element.73), channel_id=1, source_target_pairs={{0,12},{4,8},{8,4},{12,0},{16,28},{20,24},{24,20},{28,16},{1,13},{... | collective-permute-start | bytes 147464 | tf_op jit(solution)/shard_map/ppermute | solution.py:479
  40.8 11.5 %collective-permute-start.15 = (f32[32,384]{1,0:T(8,128)S(1)}, f32[32,384]{1,0:T(8,128)S(1)}, u32[]{:S(2)}, u32[]{:S(2)}) collective-permute-start(f32[32,384]{1,0:T(8,128)S(1)} %get-tuple-element.74), channel_id=1, source_target_pairs={{0,20},{4,16},{8,28},{12,24},{16,4},{20,0},{24,12},{28,8},{1,21},{... | collective-permute-start | bytes 147464 | tf_op jit(solution)/shard_map/ppermute | solution.py:479
  42.8 4.1 %collective-permute-start.20 = (f32[32,384]{1,0:T(8,128)S(1)}, f32[32,384]{1,0:T(8,128)S(1)}, u32[]{:S(2)}, u32[]{:S(2)}) collective-permute-start(f32[32,384]{1,0:T(8,128)S(1)} %get-tuple-element.81), channel_id=1, source_target_pairs={{0,8},{4,12},{8,0},{12,4},{16,24},{20,28},{24,16},{28,20},{1,9},{5... | collective-permute-start | bytes 147464 | tf_op jit(solution)/shard_map/ppermute | solution.py:479
  43.2 9.1 %collective-permute-start.18 = (f32[36,512]{1,0:T(8,128)S(1)}, f32[36,512]{1,0:T(8,128)S(1)}, u32[]{:S(2)}, u32[]{:S(2)}) collective-permute-start(f32[36,512]{1,0:T(8,128)S(1)} %get-tuple-element.79), channel_id=1, source_target_pairs={{0,1},{1,0},{2,3},{3,2},{4,5},{5,4},{6,7},{7,6},{8,9},{9,8},{10,11... | collective-permute-start | bytes 221192 | tf_op jit(solution)/shard_map/ppermute | solution.py:487
  44.2 8.1 %collective-permute-start.19 = (f32[36,512]{1,0:T(8,128)S(1)}, f32[36,512]{1,0:T(8,128)S(1)}, u32[]{:S(2)}, u32[]{:S(2)}) collective-permute-start(f32[36,512]{1,0:T(8,128)S(1)} %get-tuple-element.80), channel_id=1, source_target_pairs={{0,3},{1,2},{2,1},{3,0},{4,7},{5,6},{6,5},{7,4},{8,11},{9,10},{10,... | collective-permute-start | bytes 221192 | tf_op jit(solution)/shard_map/ppermute | solution.py:487
  46.9 5.4 %collective-permute-start.17 = (f32[64,384]{1,0:T(8,128)S(1)}, f32[64,384]{1,0:T(8,128)S(1)}, u32[]{:S(2)}, u32[]{:S(2)}) collective-permute-start(f32[64,384]{1,0:T(8,128)S(1)} %pad_maximum_fusion.2), channel_id=1, source_target_pairs={{0,4},{4,0},{8,12},{12,8},{16,20},{20,16},{24,28},{28,24},{1,5},{5... | collective-permute-start | bytes 294920 | tf_op jit(solution)/shard_map/ppermute | solution.py:479
where the time goes:
time: 54.4 us; the launch traced here: 54.2 us
  starting transfers between devices  25.9 us (48%)
  Pallas kernels  20.1 us (37%)
  waiting for transfers between devices  8.07 us (15%)
    ppermute x15, starting transfers between devices, along(): lax.ppermute(block, 'node', [(p, target_of(route, p, count)) for p in ran...  22.9 us
    pallas_call x7, Pallas kernels, call(): pl.pallas_call(functools.partial(kernel, unit=unit, **options), in_specs=...  20.1 us
    ppermute x15, waiting for transfers between devices, along(): lax.ppermute(block, 'node', [(p, target_of(route, p, count)) for p in ran...  8.05 us
    ppermute x6, starting transfers between devices, body(): lax.ppermute(x, 'freq', list(enumerate(r)))  2.93 us
  transfers between devices with their start and end apart: 21, of which 6 were waited for; matrix products, arithmetic and copies ran while one was open for 0% of the time, Pallas kernels for 25%

commit v1 on v0

--- a/solution.py
+++ b/solution.py
@@ -483,10 +483,9 @@
         arrived = {}
         for g in direct:
             arrived[g] = along(sends[g], g)
-        across = [
-            lax.ppermute(x, "freq", list(enumerate(r)))
-            for x, r in zip(sends[len(plan) :], edge_routes)
-        ]
+        across = []
+        for x, r in zip(sends[len(plan) :], edge_routes):
+            across.append(lax.ppermute(x, "freq", list(enumerate(r))))
         if relay:
             passed = jnp.concatenate([sends[relay[1]], arrived[relay[0]][width:]], axis=0)
             passed, spectra = lax.optimization_barrier((passed, spectra))

time: 54.4 us -> 54.4 us (level)
  no operation moved by 1% of the time
where the time goes in v1:
time: 54.4 us; the launch traced here: 54.2 us
  starting transfers between devices  25.9 us (48%)
  Pallas kernels  20.1 us (37%)
  waiting for transfers between devices  8.07 us (15%)
    ppermute x15, starting transfers between devices, along(): lax.ppermute(block, 'node', [(p, target_of(route, p, count)) for p in ran...  22.9 us
    pallas_call x7, Pallas kernels, call(): pl.pallas_call(functools.partial(kernel, unit=unit, **options), in_specs=...  20.1 us
    ppermute x15, waiting for transfers between devices, along(): lax.ppermute(block, 'node', [(p, target_of(route, p, count)) for p in ran...  8.05 us
    ppermute x6, starting transfers between devices, body(): across.append(lax.ppermute(x, 'freq', list(enumerate(r))))  2.93 us
  transfers between devices with their start and end apart: 21, of which 6 were waited for; matrix products, arithmetic and copies ran while one was open for 0% of the time, Pallas kernels for 25%

profile of v1, /device:TPU:0, one launch (start us, length us, event | category | flops | bytes accessed | tf_op | source)
XLA Modules:
  0.0 54.2 jit_solution(12721872382990583912)
XLA Ops:
  0.0 1.9 %shard_map.109 = (f32[64,384]{1,0:T(8,128)S(1)}, f32[32,384]{1,0:T(8,128)S(1)}, f32[32,384]{1,0:T(8,128)S(1)}, f32[32,384]{1,0:T(8,128)S(1)}, f32[32,384]{1,0:T(...) custom-call(f32[9,36,512]{2,1,0:T(8,128)} %action.1, ...), custom_call_target="tpu_custom_call" | custom-call | bytes 663552 | tf_op jit(solution)/shard_map/pallas_call | solution.py:440
  1.9 5.1 %collective-permute-start.2 = (f32[64,384]{1,0:T(8,128)S(1)}, f32[64,384]{1,0:T(8,128)S(1)}, u32[]{:S(2)}, u32[]{:S(2)}) collective-permute-start(f32[64,384]{1,0:T(8,128)S(1)} %get-tuple-element.47), channel_id=1, source_target_pairs={{0,24},{4,28},{8,16},{12,20},{16,8},{20,12},{24,0},{28,4},{1,25},{... | collective-permute-start | bytes 294920 | tf_op jit(solution)/shard_map/ppermute | solution.py:479
  7.1 0.5 collective-permute-start
  7.5 1.1 %collective-permute-start.1 = (f32[32,384]{1,0:T(8,128)S(1)}, f32[32,384]{1,0:T(8,128)S(1)}, u32[]{:S(2)}, u32[]{:S(2)}) collective-permute-start(f32[32,384]{1,0:T(8,128)S(1)} %get-tuple-element.45), channel_id=1, source_target_pairs={{0,20},{4,16},{8,28},{12,24},{16,4},{20,0},{24,12},{28,8},{1,21},{... | collective-permute-start | bytes 147464 | tf_op jit(solution)/shard_map/ppermute | solution.py:479
  8.6 1.4 %collective-permute-start.6 = (f32[32,384]{1,0:T(8,128)S(1)}, f32[32,384]{1,0:T(8,128)S(1)}, u32[]{:S(2)}, u32[]{:S(2)}) collective-permute-start(f32[32,384]{1,0:T(8,128)S(1)} %get-tuple-element.52), channel_id=1, source_target_pairs={{0,8},{4,12},{8,0},{12,4},{16,24},{20,28},{24,16},{28,20},{1,9},{5... | collective-permute-start | bytes 147464 | tf_op jit(solution)/shard_map/ppermute | solution.py:479
  10.0 0.0 collective-permute-start.4
  10.0 0.4 collective-permute-done.2.refs_0_
  10.4 1.2 %collective-permute-start.5 = (f32[36,512]{1,0:T(8,128)S(1)}, f32[36,512]{1,0:T(8,128)S(1)}, u32[]{:S(2)}, u32[]{:S(2)}) collective-permute-start(f32[36,512]{1,0:T(8,128)S(1)} %get-tuple-element.51), channel_id=1, source_target_pairs={{0,3},{1,2},{2,1},{3,0},{4,7},{5,6},{6,5},{7,4},{8,11},{9,10},{10,... | collective-permute-start | bytes 221192 | tf_op jit(solution)/shard_map/ppermute | solution.py:488
  11.7 1.9 %collective-permute-done.6.refs_1_ = f32[32,384]{1,0:T(8,128)S(1)} collective-permute-done((f32[32,384]{1,0:T(8,128)S(1)}, f32[32,384]{1,0:T(8,128)S(1)}, u32[]{:S(2)}, u32[]{:S(2)}) %collective-permute-start.6) | collective-permute-done | bytes 49184 | tf_op jit(solution)/shard_map/ppermute | solution.py:479
  13.6 1.1 %collective-permute-start.3 = (f32[64,384]{1,0:T(8,128)S(1)}, f32[64,384]{1,0:T(8,128)S(1)}, u32[]{:S(2)}, u32[]{:S(2)}) collective-permute-start(f32[64,384]{1,0:T(8,128)S(1)} %pad_maximum_fusion), channel_id=1, source_target_pairs={{0,4},{4,0},{8,12},{12,8},{16,20},{20,16},{24,28},{28,24},{1,5},{5... | collective-permute-start | bytes 294920 | tf_op jit(solution)/shard_map/ppermute | solution.py:479
  14.7 5.1 %shard_map.110 = (f32[9,36,512]{2,1,0:T(8,128)S(1)}, f32[9,36,512]{2,1,0:T(8,128)S(1)}, f32[9,36,512]{2,1,0:T(8,128)S(1)}, f32[9,36,512]{2,1,0:T(8,128)S(1)}) custom-call(f32[64,384]{1,0:T(8,128)S(1)} %collective-permute-done.2.refs_0_, f32[32,384]{1,0:T(8,128)S(1)} %collective-permute-done.6.refs_1_, f32[9,36,512]{2,1,0:T(8,128)S(1)} %get-tuple-element.53.refs_2_, ...), custom_call_target="tpu_custom_call" | custom-call | flops 3057647616 | bytes 663552 | tf_op jit(solution)/shard_map/pallas_call | solution.py:440
  19.8 0.0 collective-permute-done.refs_0_
  19.8 0.0 collective-permute-done.1.refs_1_
  19.8 0.0 collective-permute-done.4.refs_3_
  19.8 0.0 collective-permute-done.5.refs_4_
  19.8 0.0 collective-permute-done.3.refs_2_
  19.8 1.5 %shard_map.111 = (f32[9,36,512]{2,1,0:T(8,128)S(1)}, f32[64,384]{1,0:T(8,128)S(1)}, f32[32,384]{1,0:T(8,128)S(1)}, f32[32,384]{1,0:T(8,128)S(1)}, f32[32,384]{1,...) custom-call(f32[32,384]{1,0:T(8,128)S(1)} %collective-permute-done.refs_0_, ...), custom_call_target="tpu_custom_call" | custom-call | flops 679477248 | bytes 663552 | tf_op jit(solution)/shard_map/pallas_call | solution.py:440
  21.3 3.3 %collective-permute-start.9 = (f32[64,384]{1,0:T(8,128)S(1)}, f32[64,384]{1,0:T(8,128)S(1)}, u32[]{:S(2)}, u32[]{:S(2)}) collective-permute-start(f32[64,384]{1,0:T(8,128)S(1)} %get-tuple-element.65), channel_id=1, source_target_pairs={{0,24},{4,28},{8,16},{12,20},{16,8},{20,12},{24,0},{28,4},{1,25},{... | collective-permute-start | bytes 294920 | tf_op jit(solution)/shard_map/ppermute | solution.py:479
  24.6 0.0 collective-permute-start.7
  24.6 2.1 %collective-permute-start.8 = (f32[32,384]{1,0:T(8,128)S(1)}, f32[32,384]{1,0:T(8,128)S(1)}, u32[]{:S(2)}, u32[]{:S(2)}) collective-permute-start(f32[32,384]{1,0:T(8,128)S(1)} %get-tuple-element.63), channel_id=1, source_target_pairs={{0,20},{4,16},{8,28},{12,24},{16,4},{20,0},{24,12},{28,8},{1,21},{... | collective-permute-start | bytes 147464 | tf_op jit(solution)/shard_map/ppermute | solution.py:479
  26.6 0.7 %collective-permute-start.13 = (f32[32,384]{1,0:T(8,128)S(1)}, f32[32,384]{1,0:T(8,128)S(1)}, u32[]{:S(2)}, u32[]{:S(2)}) collective-permute-start(f32[32,384]{1,0:T(8,128)S(1)} %get-tuple-element.70), channel_id=1, source_target_pairs={{0,8},{4,12},{8,0},{12,4},{16,24},{20,28},{24,16},{28,20},{1,9},{5... | collective-permute-start | bytes 147464 | tf_op jit(solution)/shard_map/ppermute | solution.py:479
  27.3 0.0 collective-permute-start.11
  27.3 0.5 collective-permute-done.9.refs_0_
  27.9 1.1 %collective-permute-start.12 = (f32[36,512]{1,0:T(8,128)S(1)}, f32[36,512]{1,0:T(8,128)S(1)}, u32[]{:S(2)}, u32[]{:S(2)}) collective-permute-start(f32[36,512]{1,0:T(8,128)S(1)} %get-tuple-element.69), channel_id=1, source_target_pairs={{0,3},{1,2},{2,1},{3,0},{4,7},{5,6},{6,5},{7,4},{8,11},{9,10},{10,... | collective-permute-start | bytes 221192 | tf_op jit(solution)/shard_map/ppermute | solution.py:488
  29.0 2.0 %collective-permute-done.13.refs_1_ = f32[32,384]{1,0:T(8,128)S(1)} collective-permute-done((f32[32,384]{1,0:T(8,128)S(1)}, f32[32,384]{1,0:T(8,128)S(1)}, u32[]{:S(2)}, u32[]{:S(2)}) %collective-permute-start.13) | collective-permute-done | bytes 49184 | tf_op jit(solution)/shard_map/ppermute | solution.py:479
  31.0 0.8 %collective-permute-start.10 = (f32[64,384]{1,0:T(8,128)S(1)}, f32[64,384]{1,0:T(8,128)S(1)}, u32[]{:S(2)}, u32[]{:S(2)}) collective-permute-start(f32[64,384]{1,0:T(8,128)S(1)} %pad_maximum_fusion.1), channel_id=1, source_target_pairs={{0,4},{4,0},{8,12},{12,8},{16,20},{20,16},{24,28},{28,24},{1,5},{5... | collective-permute-start | bytes 294920 | tf_op jit(solution)/shard_map/ppermute | solution.py:479
  31.8 4.1 %shard_map.112.refs_5_ = f32[9,36,512]{2,1,0:T(8,128)S(1)} custom-call(f32[64,384]{1,0:T(8,128)S(1)} %collective-permute-done.9.refs_0_, f32[32,384]{1,0:T(8,128)S(1)} %collective-permute-done.13.refs_1_, f32[9,36,512]{2,1,0:T(8,128)S(1)} %get-tuple-element.71.refs_2_, f32[9,36,512]{2,1,0:T(8,128)S(1)} %get-tuple-element.59.refs_6_.refs_3_, ...), custom_call_target="tpu_custom_call" | custom-call | flops 3057647616 | bytes 663552 | tf_op jit(solution)/shard_map/pallas_call | solution.py:440
  36.0 0.0 collective-permute-done.7.refs_0_
  36.0 0.0 collective-permute-done.8.refs_1_
  36.0 0.0 collective-permute-done.11.refs_3_
  36.0 0.0 collective-permute-done.12.refs_4_
  36.0 0.0 collective-permute-done.10.refs_2_
  36.0 1.5 %shard_map.113 = (f32[9,36,512]{2,1,0:T(8,128)S(1)}, f32[64,384]{1,0:T(8,128)S(1)}, f32[32,384]{1,0:T(8,128)S(1)}, f32[32,384]{1,0:T(8,128)S(1)}, f32[32,384]{1,...) custom-call(f32[32,384]{1,0:T(8,128)S(1)} %collective-permute-done.7.refs_0_, ...), custom_call_target="tpu_custom_call" | custom-call | flops 679477248 | bytes 663552 | tf_op jit(solution)/shard_map/pallas_call | solution.py:440
  37.5 2.7 %collective-permute-start.16 = (f32[64,384]{1,0:T(8,128)S(1)}, f32[64,384]{1,0:T(8,128)S(1)}, u32[]{:S(2)}, u32[]{:S(2)}) collective-permute-start(f32[64,384]{1,0:T(8,128)S(1)} %get-tuple-element.76), channel_id=1, source_target_pairs={{0,24},{4,28},{8,16},{12,20},{16,8},{20,12},{24,0},{28,4},{1,25},{... | collective-permute-start | bytes 294920 | tf_op jit(solution)/shard_map/ppermute | solution.py:479
  40.2 0.6 %collective-permute-start.14 = (f32[32,384]{1,0:T(8,128)S(1)}, f32[32,384]{1,0:T(8,128)S(1)}, u32[]{:S(2)}, u32[]{:S(2)}) collective-permute-start(f32[32,384]{1,0:T(8,128)S(1)} %get-tuple-element.73), channel_id=1, source_target_pairs={{0,12},{4,8},{8,4},{12,0},{16,28},{20,24},{24,20},{28,16},{1,13},{... | collective-permute-start | bytes 147464 | tf_op jit(solution)/shard_map/ppermute | solution.py:479
  40.8 2.1 %collective-permute-start.15 = (f32[32,384]{1,0:T(8,128)S(1)}, f32[32,384]{1,0:T(8,128)S(1)}, u32[]{:S(2)}, u32[]{:S(2)}) collective-permute-start(f32[32,384]{1,0:T(8,128)S(1)} %get-tuple-element.74), channel_id=1, source_target_pairs={{0,20},{4,16},{8,28},{12,24},{16,4},{20,0},{24,12},{28,8},{1,21},{... | collective-permute-start | bytes 147464 | tf_op jit(solution)/shard_map/ppermute | solution.py:479
  42.8 0.3 collective-permute-start.20
  43.2 0.0 collective-permute-start.18
  43.2 1.0 %collective-permute-done.16.refs_0_ = f32[64,384]{1,0:T(8,128)S(1)} collective-permute-done((f32[64,384]{1,0:T(8,128)S(1)}, f32[64,384]{1,0:T(8,128)S(1)}, u32[]{:S(2)}, u32[]{:S(2)}) %collective-permute-start.16) | collective-permute-done | bytes 98336 | tf_op jit(solution)/shard_map/ppermute | solution.py:479
  44.2 0.6 %collective-permute-start.19 = (f32[36,512]{1,0:T(8,128)S(1)}, f32[36,512]{1,0:T(8,128)S(1)}, u32[]{:S(2)}, u32[]{:S(2)}) collective-permute-start(f32[36,512]{1,0:T(8,128)S(1)} %get-tuple-element.80), channel_id=1, source_target_pairs={{0,3},{1,2},{2,1},{3,0},{4,7},{5,6},{6,5},{7,4},{8,11},{9,10},{10,... | collective-permute-start | bytes 221192 | tf_op jit(solution)/shard_map/ppermute | solution.py:488
  44.8 2.1 %collective-permute-done.20.refs_1_ = f32[32,384]{1,0:T(8,128)S(1)} collective-permute-done((f32[32,384]{1,0:T(8,128)S(1)}, f32[32,384]{1,0:T(8,128)S(1)}, u32[]{:S(2)}, u32[]{:S(2)}) %collective-permute-start.20) | collective-permute-done | bytes 49184 | tf_op jit(solution)/shard_map/ppermute | solution.py:479
  46.9 1.2 %collective-permute-start.17 = (f32[64,384]{1,0:T(8,128)S(1)}, f32[64,384]{1,0:T(8,128)S(1)}, u32[]{:S(2)}, u32[]{:S(2)}) collective-permute-start(f32[64,384]{1,0:T(8,128)S(1)} %pad_maximum_fusion.2), channel_id=1, source_target_pairs={{0,4},{4,0},{8,12},{12,8},{16,20},{20,16},{24,28},{28,24},{1,5},{5... | collective-permute-start | bytes 294920 | tf_op jit(solution)/shard_map/ppermute | solution.py:479
  48.1 4.1 %shard_map.114.refs_5_ = f32[9,36,512]{2,1,0:T(8,128)S(1)} custom-call(f32[64,384]{1,0:T(8,128)S(1)} %collective-permute-done.16.refs_0_, f32[32,384]{1,0:T(8,128)S(1)} %collective-permute-done.20.refs_1_, f32[9,36,512]{2,1,0:T(8,128)S(1)} %get-tuple-element.82.refs_2_, f32[9,36,512]{2,1,0:T(8,128)S(1)} %get-tuple-element.59.refs_6_.refs_3_, ...), custom_call_target="tpu_custom_call" | custom-call | flops 3057647616 | bytes 663552 | tf_op jit(solution)/shard_map/pallas_call | solution.py:440
  52.3 0.0 collective-permute-done.14.refs_0_
  52.3 0.0 collective-permute-done.15.refs_1_
  52.3 0.0 collective-permute-done.18.refs_3_
  52.3 0.0 collective-permute-done.19.refs_4_
  52.3 0.0 collective-permute-done.17.refs_2_
  52.3 1.9 %shard_map.115 = f32[9,36,512]{2,1,0:T(8,128)} custom-call(f32[32,384]{1,0:T(8,128)S(1)} %collective-permute-done.14.refs_0_, f32[32,384]{1,0:T(8,128)S(1)} %collective-permute-done.15.refs_1_, f32[64,384]{1,0:T(8,128)S(1)} %collective-permute-done.17.refs_2_, f32[36,512]{1,0:T(8,128)S(1)} %collective-permute-done.18.refs_3_, ...), custom_call_target="tpu_custom_call" | custom-call | flops 679477248 | bytes 663552 | tf_op jit(solution)/shard_map/pallas_call | solution.py:440
  (6 shorter events, 0.0 us)
Async XLA Ops:
  1.9 8.5 %collective-permute-start.2 = (f32[64,384]{1,0:T(8,128)S(1)}, f32[64,384]{1,0:T(8,128)S(1)}, u32[]{:S(2)}, u32[]{:S(2)}) collective-permute-start(f32[64,384]{1,0:T(8,128)S(1)} %get-tuple-element.47), channel_id=1, source_target_pairs={{0,24},{4,28},{8,16},{12,20},{16,8},{20,12},{24,0},{28,4},{1,25},{... | collective-permute-start | bytes 294920 | tf_op jit(solution)/shard_map/ppermute | solution.py:479
  7.1 12.7 %collective-permute-start = (f32[32,384]{1,0:T(8,128)S(1)}, f32[32,384]{1,0:T(8,128)S(1)}, u32[]{:S(2)}, u32[]{:S(2)}) collective-permute-start(f32[32,384]{1,0:T(8,128)S(1)} %get-tuple-element.44), channel_id=1, source_target_pairs={{0,12},{4,8},{8,4},{12,0},{16,28},{20,24},{24,20},{28,16},{1,13},{... | collective-permute-start | bytes 147464 | tf_op jit(solution)/shard_map/ppermute | solution.py:479
  7.5 12.3 %collective-permute-start.1 = (f32[32,384]{1,0:T(8,128)S(1)}, f32[32,384]{1,0:T(8,128)S(1)}, u32[]{:S(2)}, u32[]{:S(2)}) collective-permute-start(f32[32,384]{1,0:T(8,128)S(1)} %get-tuple-element.45), channel_id=1, source_target_pairs={{0,20},{4,16},{8,28},{12,24},{16,4},{20,0},{24,12},{28,8},{1,21},{... | collective-permute-start | bytes 147464 | tf_op jit(solution)/shard_map/ppermute | solution.py:479
  8.6 5.0 %collective-permute-start.6 = (f32[32,384]{1,0:T(8,128)S(1)}, f32[32,384]{1,0:T(8,128)S(1)}, u32[]{:S(2)}, u32[]{:S(2)}) collective-permute-start(f32[32,384]{1,0:T(8,128)S(1)} %get-tuple-element.52), channel_id=1, source_target_pairs={{0,8},{4,12},{8,0},{12,4},{16,24},{20,28},{24,16},{28,20},{1,9},{5... | collective-permute-start | bytes 147464 | tf_op jit(solution)/shard_map/ppermute | solution.py:479
  10.0 9.8 %collective-permute-start.4 = (f32[36,512]{1,0:T(8,128)S(1)}, f32[36,512]{1,0:T(8,128)S(1)}, u32[]{:S(2)}, u32[]{:S(2)}) collective-permute-start(f32[36,512]{1,0:T(8,128)S(1)} %get-tuple-element.50), channel_id=1, source_target_pairs={{0,1},{1,0},{2,3},{3,2},{4,5},{5,4},{6,7},{7,6},{8,9},{9,8},{10,11... | collective-permute-start | bytes 221192 | tf_op jit(solution)/shard_map/ppermute | solution.py:488
  10.4 9.4 %collective-permute-start.5 = (f32[36,512]{1,0:T(8,128)S(1)}, f32[36,512]{1,0:T(8,128)S(1)}, u32[]{:S(2)}, u32[]{:S(2)}) collective-permute-start(f32[36,512]{1,0:T(8,128)S(1)} %get-tuple-element.51), channel_id=1, source_target_pairs={{0,3},{1,2},{2,1},{3,0},{4,7},{5,6},{6,5},{7,4},{8,11},{9,10},{10,... | collective-permute-start | bytes 221192 | tf_op jit(solution)/shard_map/ppermute | solution.py:488
  13.6 6.2 %collective-permute-start.3 = (f32[64,384]{1,0:T(8,128)S(1)}, f32[64,384]{1,0:T(8,128)S(1)}, u32[]{:S(2)}, u32[]{:S(2)}) collective-permute-start(f32[64,384]{1,0:T(8,128)S(1)} %pad_maximum_fusion), channel_id=1, source_target_pairs={{0,4},{4,0},{8,12},{12,8},{16,20},{20,16},{24,28},{28,24},{1,5},{5... | collective-permute-start | bytes 294920 | tf_op jit(solution)/shard_map/ppermute | solution.py:479
  21.3 6.6 %collective-permute-start.9 = (f32[64,384]{1,0:T(8,128)S(1)}, f32[64,384]{1,0:T(8,128)S(1)}, u32[]{:S(2)}, u32[]{:S(2)}) collective-permute-start(f32[64,384]{1,0:T(8,128)S(1)} %get-tuple-element.65), channel_id=1, source_target_pairs={{0,24},{4,28},{8,16},{12,20},{16,8},{20,12},{24,0},{28,4},{1,25},{... | collective-permute-start | bytes 294920 | tf_op jit(solution)/shard_map/ppermute | solution.py:479
  24.6 11.4 %collective-permute-start.7 = (f32[32,384]{1,0:T(8,128)S(1)}, f32[32,384]{1,0:T(8,128)S(1)}, u32[]{:S(2)}, u32[]{:S(2)}) collective-permute-start(f32[32,384]{1,0:T(8,128)S(1)} %get-tuple-element.62), channel_id=1, source_target_pairs={{0,12},{4,8},{8,4},{12,0},{16,28},{20,24},{24,20},{28,16},{1,13},{... | collective-permute-start | bytes 147464 | tf_op jit(solution)/shard_map/ppermute | solution.py:479
  24.6 11.4 %collective-permute-start.8 = (f32[32,384]{1,0:T(8,128)S(1)}, f32[32,384]{1,0:T(8,128)S(1)}, u32[]{:S(2)}, u32[]{:S(2)}) collective-permute-start(f32[32,384]{1,0:T(8,128)S(1)} %get-tuple-element.63), channel_id=1, source_target_pairs={{0,20},{4,16},{8,28},{12,24},{16,4},{20,0},{24,12},{28,8},{1,21},{... | collective-permute-start | bytes 147464 | tf_op jit(solution)/shard_map/ppermute | solution.py:479
  26.6 4.3 %collective-permute-start.13 = (f32[32,384]{1,0:T(8,128)S(1)}, f32[32,384]{1,0:T(8,128)S(1)}, u32[]{:S(2)}, u32[]{:S(2)}) collective-permute-start(f32[32,384]{1,0:T(8,128)S(1)} %get-tuple-element.70), channel_id=1, source_target_pairs={{0,8},{4,12},{8,0},{12,4},{16,24},{20,28},{24,16},{28,20},{1,9},{5... | collective-permute-start | bytes 147464 | tf_op jit(solution)/shard_map/ppermute | solution.py:479
  27.3 8.7 %collective-permute-start.11 = (f32[36,512]{1,0:T(8,128)S(1)}, f32[36,512]{1,0:T(8,128)S(1)}, u32[]{:S(2)}, u32[]{:S(2)}) collective-permute-start(f32[36,512]{1,0:T(8,128)S(1)} %get-tuple-element.68), channel_id=1, source_target_pairs={{0,1},{1,0},{2,3},{3,2},{4,5},{5,4},{6,7},{7,6},{8,9},{9,8},{10,11... | collective-permute-start | bytes 221192 | tf_op jit(solution)/shard_map/ppermute | solution.py:488
  27.9 8.1 %collective-permute-start.12 = (f32[36,512]{1,0:T(8,128)S(1)}, f32[36,512]{1,0:T(8,128)S(1)}, u32[]{:S(2)}, u32[]{:S(2)}) collective-permute-start(f32[36,512]{1,0:T(8,128)S(1)} %get-tuple-element.69), channel_id=1, source_target_pairs={{0,3},{1,2},{2,1},{3,0},{4,7},{5,6},{6,5},{7,4},{8,11},{9,10},{10,... | collective-permute-start | bytes 221192 | tf_op jit(solution)/shard_map/ppermute | solution.py:488
  31.0 5.0 %collective-permute-start.10 = (f32[64,384]{1,0:T(8,128)S(1)}, f32[64,384]{1,0:T(8,128)S(1)}, u32[]{:S(2)}, u32[]{:S(2)}) collective-permute-start(f32[64,384]{1,0:T(8,128)S(1)} %pad_maximum_fusion.1), channel_id=1, source_target_pairs={{0,4},{4,0},{8,12},{12,8},{16,20},{20,16},{24,28},{28,24},{1,5},{5... | collective-permute-start | bytes 294920 | tf_op jit(solution)/shard_map/ppermute | solution.py:479
  37.5 6.7 %collective-permute-start.16 = (f32[64,384]{1,0:T(8,128)S(1)}, f32[64,384]{1,0:T(8,128)S(1)}, u32[]{:S(2)}, u32[]{:S(2)}) collective-permute-start(f32[64,384]{1,0:T(8,128)S(1)} %get-tuple-element.76), channel_id=1, source_target_pairs={{0,24},{4,28},{8,16},{12,20},{16,8},{20,12},{24,0},{28,4},{1,25},{... | collective-permute-start | bytes 294920 | tf_op jit(solution)/shard_map/ppermute | solution.py:479
  40.2 12.1 %collective-permute-start.14 = (f32[32,384]{1,0:T(8,128)S(1)}, f32[32,384]{1,0:T(8,128)S(1)}, u32[]{:S(2)}, u32[]{:S(2)}) collective-permute-start(f32[32,384]{1,0:T(8,128)S(1)} %get-tuple-element.73), channel_id=1, source_target_pairs={{0,12},{4,8},{8,4},{12,0},{16,28},{20,24},{24,20},{28,16},{1,13},{... | collective-permute-start | bytes 147464 | tf_op jit(solution)/shard_map/ppermute | solution.py:479
  40.8 11.5 %collective-permute-start.15 = (f32[32,384]{1,0:T(8,128)S(1)}, f32[32,384]{1,0:T(8,128)S(1)}, u32[]{:S(2)}, u32[]{:S(2)}) collective-permute-start(f32[32,384]{1,0:T(8,128)S(1)} %get-tuple-element.74), channel_id=1, source_target_pairs={{0,20},{4,16},{8,28},{12,24},{16,4},{20,0},{24,12},{28,8},{1,21},{... | collective-permute-start | bytes 147464 | tf_op jit(solution)/shard_map/ppermute | solution.py:479
  42.8 4.1 %collective-permute-start.20 = (f32[32,384]{1,0:T(8,128)S(1)}, f32[32,384]{1,0:T(8,128)S(1)}, u32[]{:S(2)}, u32[]{:S(2)}) collective-permute-start(f32[32,384]{1,0:T(8,128)S(1)} %get-tuple-element.81), channel_id=1, source_target_pairs={{0,8},{4,12},{8,0},{12,4},{16,24},{20,28},{24,16},{28,20},{1,9},{5... | collective-permute-start | bytes 147464 | tf_op jit(solution)/shard_map/ppermute | solution.py:479
  43.2 9.1 %collective-permute-start.18 = (f32[36,512]{1,0:T(8,128)S(1)}, f32[36,512]{1,0:T(8,128)S(1)}, u32[]{:S(2)}, u32[]{:S(2)}) collective-permute-start(f32[36,512]{1,0:T(8,128)S(1)} %get-tuple-element.79), channel_id=1, source_target_pairs={{0,1},{1,0},{2,3},{3,2},{4,5},{5,4},{6,7},{7,6},{8,9},{9,8},{10,11... | collective-permute-start | bytes 221192 | tf_op jit(solution)/shard_map/ppermute | solution.py:488
  44.2 8.1 %collective-permute-start.19 = (f32[36,512]{1,0:T(8,128)S(1)}, f32[36,512]{1,0:T(8,128)S(1)}, u32[]{:S(2)}, u32[]{:S(2)}) collective-permute-start(f32[36,512]{1,0:T(8,128)S(1)} %get-tuple-element.80), channel_id=1, source_target_pairs={{0,3},{1,2},{2,1},{3,0},{4,7},{5,6},{6,5},{7,4},{8,11},{9,10},{10,... | collective-permute-start | bytes 221192 | tf_op jit(solution)/shard_map/ppermute | solution.py:488
  46.9 5.4 %collective-permute-start.17 = (f32[64,384]{1,0:T(8,128)S(1)}, f32[64,384]{1,0:T(8,128)S(1)}, u32[]{:S(2)}, u32[]{:S(2)}) collective-permute-start(f32[64,384]{1,0:T(8,128)S(1)} %pad_maximum_fusion.2), channel_id=1, source_target_pairs={{0,4},{4,0},{8,12},{12,8},{16,20},{20,16},{24,28},{28,24},{1,5},{5... | collective-permute-start | bytes 294920 | tf_op jit(solution)/shard_map/ppermute | solution.py:479
